TPU v7x, 32 devices: a whole 2x2x4 slice. The times are simulated.
32 devices in a mesh: seq: 8 (over z, y), head: 4 (over x, core).
Axes of the slice: x: 2, y: 2, z: 4, core: 2. Of those that a mesh axis runs over, the one named last changes fastest.
Arguments:
- hidden_states: bfloat16 [8, 512, 3584], P(None, 'seq', 'head'), may hold values from -6 to 6
- boundary: int32 [8, 64], replicated, may hold values from 0 to 511, as said below
- valid: int32 [8, 64], replicated, may hold values from 0 to 1, as said below
- pairs: int32 [8, 2], replicated, may hold values from 0 to 7, as said below
- w_first: bfloat16 [3584, 4096], P('seq', 'head'), may hold values from -0.09375 to 0.09375
- b_first: float32 [4096], P('head'), may hold values from -3 to 3
- w_second: float32 [4096], P('head'), may hold values from -0.09375 to 0.09375
Outputs:
- step_reward: float32 [8, 64], replicated
- trace_score: float32 [8], replicated
- margin: float32 [8], replicated
Inputs may be any that keep to these rules, and one draw needn't show every extreme that they name: Within a trace the 64 boundary positions are distinct and increasing. In each trace the ones come first; every trace has 16 to 64 valid steps. `pairs`: the two traces of a pair differ.
All inputs are finite; a program needn't handle non-finite values.
Results may differ from a plain program's by a relative error of at most 0.0003.
Values may be sent and summed in bfloat16 or wider, within the bound.
A program may use at most 64 MiB of HBM per device.

v0:
```python
import jax
import jax.numpy as jnp
from jax import lax
from jax.sharding import PartitionSpec as P


def score_rows(rows, w_first, b_first, w_second):
    pre = jnp.dot(
        rows, lax.all_gather(w_first, "seq", axis=0, tiled=True), preferred_element_type=jnp.float32
    )
    return jnp.sum(jnp.maximum(pre + b_first, 0.0) * w_second, axis=-1)


def per_device(hidden_states, boundary, valid, pairs, w_first, b_first, w_second):
    traces, tok_dev, quarter = hidden_states.shape
    offset = lax.axis_index("seq") * tok_dev
    positions = offset + jnp.arange(tok_dev, dtype=jnp.int32)
    hits = boundary[:, :, None] == positions[None, None, :]
    whole = lax.all_gather(hidden_states, "head", axis=2, tiled=True)
    token_logit = score_rows(
        whole.reshape(traces * tok_dev, whole.shape[2]), w_first, b_first, w_second
    )
    token_logit = token_logit.reshape(traces, tok_dev)
    partial_logit = jnp.sum(jnp.where(hits, token_logit[:, None, :], 0.0), axis=2)
    logit = lax.psum(partial_logit, ("seq", "head"))
    live = valid == 1
    step_reward = jnp.where(live, logit, jnp.float32(0.0))
    trace_score = jnp.min(jnp.where(live, logit, jnp.float32(1e30)), axis=1)
    trace_ids = jnp.arange(traces, dtype=jnp.int32)[None, :]
    winner = jnp.sum(jnp.where(pairs[:, 0:1] == trace_ids, trace_score[None, :], 0.0), axis=1)
    loser = jnp.sum(jnp.where(pairs[:, 1:2] == trace_ids, trace_score[None, :], 0.0), axis=1)
    return (step_reward, trace_score, winner - loser)


def solution(mesh):
    placed = (P(None, "seq", "head"), P(), P(), P(), P("seq", "head"), P("head"), P("head"))
    return jax.shard_map(
        per_device, mesh=mesh, in_specs=placed, out_specs=(P(), P(), P()), check_vma=False
    )
```

profile of v0, /device:TPU:0, one launch (start us, length us, event | category | flops | bytes accessed | tf_op | source)
XLA Modules:
  0.0 212.7 jit_solution(10916989333486681788)
XLA Ops:
  7.2 0.0 all-gather.3.cloned.1.call-start
  7.2 0.7 all-gather.3.cloned.1.call-update
  7.9 0.0 all-gather.5.cloned.1.call-start
  7.9 0.7 all-gather.5.cloned.1.call-update
  8.7 0.8 slice_bitcast_fusion.1
  9.4 34.3 %all-gather.3.cloned.1.call-done = bf16[8,64,3584]{2,1,0:T(8,128)(2,1)} async-done(((bf16[8,64,896]{2,1,0:T(8,128)(2,1)}), bf16[8,64,3584]{2,1,0:T(8,128)(2,1)}) %all-gather.3.cloned.1.call-update) | async-done | bytes 3670032 | tf_op jit(solution)/shard_map/all_gather | solution.py:19
  43.8 113.7 %all-gather.5.cloned.1.call-done = bf16[3584,1024]{1,0:T(8,128)(2,1)} async-done(((bf16[448,1024]{1,0:T(8,128)(2,1)}), bf16[3584,1024]{1,0:T(8,128)(2,1)}) %all-gather.5.cloned.1.call-update) | async-done | bytes 7340048 | tf_op jit(solution)/shard_map/all_gather | solution.py:9
  157.5 0.0 copy-start
  157.5 0.0 copy-start.1
  157.5 8.2 %multiply_reduce_fusion = f32[512]{0:T(512)S(1)} fusion(bf16[512,3584]{1,0:T(8,128)(2,1)} %bitcast.7, bf16[3584,1024]{1,0:T(8,128)(2,1)} %all-gather.5.cloned.1.call-done, f32[1024]{0:T(1024)} %param.13, f32[1024]{0:T(1024)} %param.12), kind=kOutput, calls=%fused_computation | convolution fusion | flops 3760193024 | bytes 11020288 | tf_op jit(solution)/shard_map/dot_general | solution.py:8
  165.7 0.1 broadcast_in_dim.44
  165.7 0.0 copy-done
  165.7 0.3 select_reduce_fusion
  166.0 38.4 %psum.7 = f32[8,64]{1,0:T(8,128)S(1)} all-reduce(f32[8,64]{1,0:T(8,128)S(1)} %select_reduce_fusion), channel_id=1, replica_groups=mesh['seq'=8,'head'=4] {'seq','head'}, use_global_device_ids=true, to_apply=%region_2.3 | all-reduce | flops 512 | bytes 4096 | tf_op jit(solution)/shard_map/psum | solution.py:25
  204.4 0.0 copy-done.1
  204.4 0.1 select_reduce_fusion.3
  204.5 0.0 copy-start.2
  204.5 0.6 broadcast_select_fusion
  205.1 0.2 select_reduce_fusion.1
  205.4 0.5 sub.3
  205.9 0.0 copy-done.2
  (1 shorter events, 0.0 us)
Async XLA Ops:
  7.2 36.6 %all-gather.3.cloned.1.call-start = ((), (), s32[]{:S(2)}) async-start(), calls=%async_computation | async-start | bytes 4587520 | tf_op jit(solution)/shard_map/all_gather | solution.py:19
  7.9 149.6 %all-gather.5.cloned.1.call-start = ((), (), s32[]{:S(2)}) async-start(), calls=%async_computation.1 | async-start | bytes 8257536 | tf_op jit(solution)/shard_map/all_gather | solution.py:9
  157.5 8.3 %copy-start = (s32[8,64]{1,0:T(8,128)S(1)}, s32[8,64]{1,0:T(8,128)}, u32[]{:S(2)}) copy-start(s32[8,64]{1,0:T(8,128)} %param.8) | copy-start | bytes 6148
  157.5 47.0 %copy-start.1 = (s32[8,64]{1,0:T(8,128)S(1)}, s32[8,64]{1,0:T(8,128)}, u32[]{:S(2)}) copy-start(s32[8,64]{1,0:T(8,128)} %param.9) | copy-start | bytes 6148
  204.5 1.3 copy-start.2
Sparse Core Ops, SparseCore 0:
  9.5 34.1 all-gather.2
  45.9 111.4 all-gather.4
where the time goes:
time: 213 us
  waiting for transfers between devices  149 us (70%)
  blocking collectives  38.4 us (18%)
  between operations  14.1 us (7%)
  matrix products  8.19 us (4%)
    all_gather x1, waiting for transfers between devices, score_rows(): lax.all_gather(w_first, 'seq', axis=0, tiled=True)  114 us
    psum x1, blocking collectives, per_device(): logit = lax.psum(partial_logit, ('seq', 'head'))  38.4 us
    all_gather x1, waiting for transfers between devices, per_device(): whole = lax.all_gather(hidden_states, 'head', axis=2, tiled=True)  34.3 us
    dot_general x1, matrix products, score_rows(): jnp.dot(rows, lax.all_gather(w_first, 'seq', axis=0, tiled=True), preferr...  8.19 us
  transfers between devices with their start and end apart: 2, of which 2 were waited for; matrix products, arithmetic and copies ran while one was open for 0% of the time, Pallas kernels for 0%

commit v1 on v0

--- a/solution.py
+++ b/solution.py
@@ -2,6 +2,10 @@
 import jax.numpy as jnp
 from jax import lax
 from jax.sharding import PartitionSpec as P
+
+
+def choose_the_columns(inner_x, a_name):
+    return jnp.concatenate(jax.lax.all_gather(inner_x, a_name), axis=2)
 
 
 def score_rows(rows, w_first, b_first, w_second):
@@ -16,7 +20,7 @@
     offset = lax.axis_index("seq") * tok_dev
     positions = offset + jnp.arange(tok_dev, dtype=jnp.int32)
     hits = boundary[:, :, None] == positions[None, None, :]
-    whole = lax.all_gather(hidden_states, "head", axis=2, tiled=True)
+    whole = choose_the_columns(hidden_states, "head")
     token_logit = score_rows(
         whole.reshape(traces * tok_dev, whole.shape[2]), w_first, b_first, w_second
     )

time: 213 us -> 213 us (level)
  local copies, waits for them, and re-layouts: 0.85 us -> 8.24 us
  waiting for transfers between devices: 149 us -> 142 us
    all_gather x1, waiting for transfers between devices: 114 us -> 106 us  [score_rows(): lax.all_gather(w_first, 'seq', axis=0, tiled=True)]
    all_gather x0 -> x1, local copies, waits for them, and re-layouts: none -> 4.87 us  [choose_the_columns(): return jnp.concatenate(jax.lax.all_gather(inner_x, a_name), axis=2)]
    unnamed x6 -> x11, local copies, waits for them, and re-layouts: 0.01 us -> 2.53 us
  transfers between devices with their start and end apart: 2 -> 2, of which waited for: 2 -> 2; matrix products, arithmetic and copies ran while one was open for 0% -> 4% of each run, Pallas kernels for 0% -> 0%
where the time goes in v1:
time: 213 us
  waiting for transfers between devices  142 us (67%)
  blocking collectives  38.4 us (18%)
  between operations  14.1 us (7%)
  matrix products  8.26 us (4%)
  local copies, waits for them, and re-layouts  8.24 us (4%)
    all_gather x1, waiting for transfers between devices, score_rows(): lax.all_gather(w_first, 'seq', axis=0, tiled=True)  106 us
    psum x1, blocking collectives, per_device(): logit = lax.psum(partial_logit, ('seq', 'head'))  38.4 us
    all_gather x1, waiting for transfers between devices, choose_the_columns(): return jnp.concatenate(jax.lax.all_gather(inner_x, a_name), axis=2)  34.3 us
    dot_general x1, matrix products, score_rows(): jnp.dot(rows, lax.all_gather(w_first, 'seq', axis=0, tiled=True), preferr...  8.26 us
    all_gather x1, local copies, waits for them, and re-layouts, choose_the_columns(): return jnp.concatenate(jax.lax.all_gather(inner_x, a_name), axis=2)  4.87 us
  transfers between devices with their start and end apart: 2, of which 2 were waited for; matrix products, arithmetic and copies ran while one was open for 4% of the time, Pallas kernels for 0%

profile of v1, /device:TPU:0, one launch (start us, length us, event | category | flops | bytes accessed | tf_op | source)
XLA Modules:
  0.0 212.8 jit_solution(2515664572823742180)
XLA Ops:
  7.2 0.0 all-gather.6.cloned.1.call-start
  7.2 0.7 all-gather.6.cloned.1.call-update
  7.9 0.0 all-gather.4.cloned.1.call-start
  7.9 0.7 all-gather.4.cloned.1.call-update
  8.7 0.8 slice_bitcast_fusion.1
  9.4 34.3 %all-gather.6.cloned.1.call-done = bf16[32,64,896]{2,1,0:T(8,128)(2,1)} async-done(((bf16[8,64,896]{2,1,0:T(8,128)(2,1)}), bf16[32,64,896]{2,1,0:T(8,128)(2,1)}) %all-gather.6.cloned.1.call-update) | async-done | bytes 3670032 | tf_op jit(solution)/shard_map/all_gather | solution.py:8
  43.8 4.9 %copy.12 = bf16[4,8,64,896]{3,0,2,1:T(4,128)(2,1)S(1)} copy(bf16[4,8,64,896]{3,2,1,0:T(8,128)(2,1)} %bitcast.12) | data formatting | bytes 7340032 | tf_op jit(solution)/shard_map/all_gather | solution.py:8
  48.6 0.0 copy-start.3
  48.7 0.0 copy-start.4
  48.7 2.5 %copy.13 = bf16[64,8,4,896]{3,1,2,0:T(8,128)(2,1)} copy(bf16[64,8,4,896]{3,2,1,0:T(4,128)(2,1)S(1)} %bitcast.11) | data formatting | bytes 7340032
  51.2 106.3 %all-gather.4.cloned.1.call-done = bf16[3584,1024]{1,0:T(8,128)(2,1)} async-done(((bf16[448,1024]{1,0:T(8,128)(2,1)}), bf16[3584,1024]{1,0:T(8,128)(2,1)}) %all-gather.4.cloned.1.call-update) | async-done | bytes 7340048 | tf_op jit(solution)/shard_map/all_gather | solution.py:13
  157.5 0.0 copy-done.3
  157.5 0.0 copy-done.4
  157.5 0.0 copy-start
  157.5 0.0 copy-start.1
  157.5 8.3 %multiply_reduce_fusion = f32[512]{0:T(512)S(1)} fusion(bf16[512,3584]{1,0:T(8,128)(2,1)} %bitcast.13, bf16[3584,1024]{1,0:T(8,128)(2,1)} %all-gather.4.cloned.1.call-done, f32[1024]{0:T(1024)S(1)} %copy-done.3, f32[1024]{0:T(1024)S(1)} %copy-done.4), kind=kOutput, calls=%fused_computation | convolution fusion | flops 3760193024 | bytes 11020288 | tf_op jit(solution)/shard_map/dot_general | solution.py:12
  165.8 0.1 broadcast_in_dim.44
  165.8 0.0 copy-done
  165.8 0.3 select_reduce_fusion
  166.1 38.4 %psum.7 = f32[8,64]{1,0:T(8,128)S(1)} all-reduce(f32[8,64]{1,0:T(8,128)S(1)} %select_reduce_fusion), channel_id=1, replica_groups=mesh['seq'=8,'head'=4] {'seq','head'}, use_global_device_ids=true, to_apply=%region_2.3 | all-reduce | flops 512 | bytes 4096 | tf_op jit(solution)/shard_map/psum | solution.py:29
  204.5 0.0 copy-done.1
  204.5 0.1 select_reduce_fusion.3
  204.6 0.0 copy-start.2
  204.6 0.6 broadcast_select_fusion
  205.2 0.2 select_reduce_fusion.1
  205.4 0.5 sub.3
  206.0 0.0 copy-done.2
  (1 shorter events, 0.0 us)
Async XLA Ops:
  7.2 36.6 %all-gather.6.cloned.1.call-start = ((), (), s32[]{:S(2)}) async-start(), calls=%async_computation.1 | async-start | bytes 4587520 | tf_op jit(solution)/shard_map/all_gather | solution.py:8
  7.9 149.6 %all-gather.4.cloned.1.call-start = ((), (), s32[]{:S(2)}) async-start(), calls=%async_computation | async-start | bytes 8257536 | tf_op jit(solution)/shard_map/all_gather | solution.py:13
  48.6 108.8 %copy-start.3 = (f32[1024]{0:T(1024)S(1)}, f32[1024]{0:T(1024)}, u32[]{:S(2)}) copy-start(f32[1024]{0:T(1024)} %param.13) | copy-start | bytes 12292
  48.7 108.8 %copy-start.4 = (f32[1024]{0:T(1024)S(1)}, f32[1024]{0:T(1024)}, u32[]{:S(2)}) copy-start(f32[1024]{0:T(1024)} %param.12) | copy-start | bytes 12292
  157.5 8.3 %copy-start = (s32[8,64]{1,0:T(8,128)S(1)}, s32[8,64]{1,0:T(8,128)}, u32[]{:S(2)}) copy-start(s32[8,64]{1,0:T(8,128)} %param.8) | copy-start | bytes 6148
  157.5 47.0 %copy-start.1 = (s32[8,64]{1,0:T(8,128)S(1)}, s32[8,64]{1,0:T(8,128)}, u32[]{:S(2)}) copy-start(s32[8,64]{1,0:T(8,128)} %param.9) | copy-start | bytes 6148
  204.6 1.3 copy-start.2
Sparse Core Ops, SparseCore 0:
  9.5 34.1 all-gather.5
  46.0 111.4 all-gather.3

commit v2 on v0

--- a/solution.py
+++ b/solution.py
@@ -2,6 +2,12 @@
 import jax.numpy as jnp
 from jax import lax
 from jax.sharding import PartitionSpec as P
+
+
+def run_hubs_on_mesh(in_array, ax_name, comm_axis):
+    for b in (comm_axis, ax_name):
+        in_array = jax.lax.psum(in_array, b)
+    return in_array
 
 
 def score_rows(rows, w_first, b_first, w_second):
@@ -22,7 +28,7 @@
     )
     token_logit = token_logit.reshape(traces, tok_dev)
     partial_logit = jnp.sum(jnp.where(hits, token_logit[:, None, :], 0.0), axis=2)
-    logit = lax.psum(partial_logit, ("seq", "head"))
+    logit = run_hubs_on_mesh(partial_logit, "seq", "head")
     live = valid == 1
     step_reward = jnp.where(live, logit, jnp.float32(0.0))
     trace_score = jnp.min(jnp.where(live, logit, jnp.float32(1e30)), axis=1)

time: 213 us -> 200 us (0.939)
  blocking collectives: 38.4 us -> 25.4 us
    psum x1 -> x2, blocking collectives: 38.4 us -> 25.4 us  [run_hubs_on_mesh(): in_array = jax.lax.psum(in_array, b)]
where the time goes in v2:
time: 200 us
  waiting for transfers between devices  149 us (74%)
  blocking collectives  25.4 us (13%)
  between operations  14.1 us (7%)
  matrix products  8.19 us (4%)
    all_gather x1, waiting for transfers between devices, score_rows(): lax.all_gather(w_first, 'seq', axis=0, tiled=True)  114 us
    all_gather x1, waiting for transfers between devices, per_device(): whole = lax.all_gather(hidden_states, 'head', axis=2, tiled=True)  34.3 us
    psum x2, blocking collectives, run_hubs_on_mesh(): in_array = jax.lax.psum(in_array, b)  25.4 us
    dot_general x1, matrix products, score_rows(): jnp.dot(rows, lax.all_gather(w_first, 'seq', axis=0, tiled=True), preferr...  8.19 us
  transfers between devices with their start and end apart: 2, of which 2 were waited for; matrix products, arithmetic and copies ran while one was open for 0% of the time, Pallas kernels for 0%

profile of v2, /device:TPU:0, one launch (start us, length us, event | category | flops | bytes accessed | tf_op | source)
XLA Modules:
  0.0 199.7 jit_solution(10876605371150894530)
XLA Ops:
  7.2 0.0 all-gather.3.cloned.1.call-start
  7.2 0.7 all-gather.3.cloned.1.call-update
  7.9 0.0 all-gather.5.cloned.1.call-start
  7.9 0.7 all-gather.5.cloned.1.call-update
  8.7 0.8 slice_bitcast_fusion.1
  9.4 34.3 %all-gather.3.cloned.1.call-done = bf16[8,64,3584]{2,1,0:T(8,128)(2,1)} async-done(((bf16[8,64,896]{2,1,0:T(8,128)(2,1)}), bf16[8,64,3584]{2,1,0:T(8,128)(2,1)}) %all-gather.3.cloned.1.call-update) | async-done | bytes 3670032 | tf_op jit(solution)/shard_map/all_gather | solution.py:25
  43.8 113.7 %all-gather.5.cloned.1.call-done = bf16[3584,1024]{1,0:T(8,128)(2,1)} async-done(((bf16[448,1024]{1,0:T(8,128)(2,1)}), bf16[3584,1024]{1,0:T(8,128)(2,1)}) %all-gather.5.cloned.1.call-update) | async-done | bytes 7340048 | tf_op jit(solution)/shard_map/all_gather | solution.py:15
  157.5 0.0 copy-start
  157.5 0.0 copy-start.1
  157.5 8.2 %multiply_reduce_fusion = f32[512]{0:T(512)S(1)} fusion(bf16[512,3584]{1,0:T(8,128)(2,1)} %bitcast.7, bf16[3584,1024]{1,0:T(8,128)(2,1)} %all-gather.5.cloned.1.call-done, f32[1024]{0:T(1024)} %param.13, f32[1024]{0:T(1024)} %param.12), kind=kOutput, calls=%fused_computation | convolution fusion | flops 3760193024 | bytes 11020288 | tf_op jit(solution)/shard_map/dot_general | solution.py:14
  165.7 0.1 broadcast_in_dim.44
  165.7 0.0 copy-done
  165.7 0.3 select_reduce_fusion
  166.0 5.7 %psum.14 = f32[8,64]{1,0:T(8,128)S(1)} all-reduce(f32[8,64]{1,0:T(8,128)S(1)} %select_reduce_fusion), channel_id=1, replica_groups=mesh['seq'=8,'head'=4] {'head'}, use_global_device_ids=true, to_apply=%region_2.3 | all-reduce | flops 512 | bytes 4096 | tf_op jit(solution)/shard_map/psum | solution.py:9
  171.7 19.7 %psum.15 = f32[8,64]{1,0:T(8,128)S(1)} all-reduce(f32[8,64]{1,0:T(8,128)S(1)} %psum.14), channel_id=1, replica_groups=mesh['seq'=8,'head'=4] {'seq'}, use_global_device_ids=true, to_apply=%region_3.4 | all-reduce | flops 512 | bytes 4096 | tf_op jit(solution)/shard_map/psum | solution.py:9
  191.4 0.0 copy-done.1
  191.4 0.1 select_reduce_fusion.3
  191.5 0.0 copy-start.2
  191.5 0.6 broadcast_select_fusion
  192.1 0.2 select_reduce_fusion.1
  192.3 0.5 sub.3
  192.9 0.0 copy-done.2
  (1 shorter events, 0.0 us)
Async XLA Ops:
  7.2 36.6 %all-gather.3.cloned.1.call-start = ((), (), s32[]{:S(2)}) async-start(), calls=%async_computation | async-start | bytes 4587520 | tf_op jit(solution)/shard_map/all_gather | solution.py:25
  7.9 149.6 %all-gather.5.cloned.1.call-start = ((), (), s32[]{:S(2)}) async-start(), calls=%async_computation.1 | async-start | bytes 8257536 | tf_op jit(solution)/shard_map/all_gather | solution.py:15
  157.5 8.3 %copy-start = (s32[8,64]{1,0:T(8,128)S(1)}, s32[8,64]{1,0:T(8,128)}, u32[]{:S(2)}) copy-start(s32[8,64]{1,0:T(8,128)} %param.8) | copy-start | bytes 6148
  157.5 33.9 %copy-start.1 = (s32[8,64]{1,0:T(8,128)S(1)}, s32[8,64]{1,0:T(8,128)}, u32[]{:S(2)}) copy-start(s32[8,64]{1,0:T(8,128)} %param.9) | copy-start | bytes 6148
  191.5 1.3 copy-start.2
Sparse Core Ops, SparseCore 0:
  9.5 34.1 all-gather.2
  45.9 111.4 all-gather.4
